TPU v7x, 128 devices: a whole 4x4x4 slice. The times are simulated.
128 devices in a mesh: row: 8 (over z, x_lo), col: 16 (over y, x_hi, core).
Axes of the slice: x: 4 (x_hi: 2, x_lo: 2; x = x_hi * 2 + x_lo), y: 4, z: 4, core: 2. Of those that a mesh axis runs over, the one named last changes fastest.
Arguments:
- tokens: bfloat16 [2048, 8192], P('row', 'col'), may hold values from -6 to 6
- gate_frozen_weight: bfloat16 [8192, 28672], P('col', 'row'), may hold values from -0.0625 to 0.0625
- gate_left_factor: bfloat16 [8192, 64], P('col'), may hold values from -0.046875 to 0.046875
- gate_right_factor: bfloat16 [64, 28672], P(None, 'row'), may hold values from -0.75 to 0.75
- gate_column_magnitude: float32 [28672], P('row'), may hold values from 0.5 to 1.5
- up_frozen_weight: bfloat16 [8192, 28672], P('col', 'row'), may hold values from -0.0625 to 0.0625
- up_left_factor: bfloat16 [8192, 64], P('col'), may hold values from -0.046875 to 0.046875
- up_right_factor: bfloat16 [64, 28672], P(None, 'row'), may hold values from -0.75 to 0.75
- up_column_magnitude: float32 [28672], P('row'), may hold values from 0.5 to 1.5
- down_frozen_weight: bfloat16 [28672, 8192], P('row', 'col'), may hold values from -0.03125 to 0.03125
- down_left_factor: bfloat16 [28672, 64], P('row'), may hold values from -0.02734375 to 0.02734375
- down_right_factor: bfloat16 [64, 8192], P(None, 'col'), may hold values from -0.75 to 0.75
- down_column_magnitude: float32 [8192], P('col'), may hold values from 0.5 to 1.5
Outputs:
- mixed: bfloat16 [2048, 8192], P('row', 'col')
All inputs are finite; a program needn't handle non-finite values.
Results may differ from a plain program's by a relative error of at most 0.028.
Values may be sent and summed in bfloat16 or wider, within the bound.
A program may use at most 192 MiB of HBM per device.

v0:
```python
import jax
import jax.numpy as jnp
from jax import lax
from jax.sharding import PartitionSpec as P

stability_offset = 1e-06


def joined_along(tiles, dim):
    shape = list(tiles.shape[1:])
    shape[dim] *= tiles.shape[0]
    return jnp.moveaxis(tiles, 0, dim).reshape(shape)


def from_everyone(value, axis):
    copies = jnp.broadcast_to(value, (lax.axis_size(axis), *value.shape))
    return lax.all_to_all(copies, axis, split_axis=0, concat_axis=0, tiled=True)


def collect(value, axis, dim):
    return joined_along(from_everyone(value, axis), dim)


def taken_together(value, axis):
    return from_everyone(value, axis).sum(axis=0)


def together(arrays, axis):
    ravelled, at, done = (jnp.concatenate([a.reshape(-1) for a in arrays]), 0, [])
    so_far = taken_together(ravelled, axis)
    for a in arrays:
        done.append(so_far[at : at + a.size].reshape(a.shape))
        at += a.size
    return tuple(done)


def sent_together(arrays, axis, dim, along):
    both = jnp.concatenate(arrays, axis=along)
    filled, at, done = (lax.psum_scatter(both, axis, scatter_dimension=dim, tiled=True), 0, [])
    for a in arrays:
        done.append(lax.slice_in_dim(filled, at, at + a.shape[along], axis=along))
        at += a.shape[along]
    return tuple(done)


def cut_along(value, dim, size):
    before, after = (value.shape[:dim], value.shape[dim + 1 :])
    return jnp.moveaxis(value.reshape(*before, size, -1, *after), dim, 0)


def sum_at_owner(value, axis, dim):
    size = lax.axis_size(axis)
    tiles = lax.all_to_all(cut_along(value, dim, size), axis, 0, 0, tiled=True)
    return jnp.sum(tiles.astype(jnp.float32), axis=0)


def column_square_totals(weight, low_b, low_a):
    merged = weight.astype(jnp.float32) + jnp.dot(low_b, low_a, preferred_element_type=jnp.float32)
    return jnp.sum(merged * merged, axis=0)


def plain_term(inputs, weight):
    return jnp.dot(inputs, weight, preferred_element_type=jnp.float32)


def rank_update_term(inputs, weight, low_b, low_a):
    value = jnp.dot(inputs, weight, preferred_element_type=jnp.float32)
    coords = jnp.dot(inputs, low_b, preferred_element_type=jnp.float32)
    return value + jnp.dot(coords, low_a.astype(jnp.float32), precision=lax.Precision.HIGHEST)


def shards(
    tokens,
    gate_frozen_weight,
    gate_left_factor,
    gate_right_factor,
    gate_column_magnitude,
    up_frozen_weight,
    up_left_factor,
    up_right_factor,
    up_column_magnitude,
    down_frozen_weight,
    down_left_factor,
    down_right_factor,
    down_column_magnitude,
):
    token_rows_full = collect(tokens, "row", 0)
    gate_sq, up_sq = together(
        (
            column_square_totals(gate_frozen_weight, gate_left_factor, gate_right_factor),
            column_square_totals(up_frozen_weight, up_left_factor, up_right_factor),
        ),
        "col",
    )
    down_squared = taken_together(
        column_square_totals(down_frozen_weight, down_left_factor, down_right_factor), "row"
    )
    gate_column_scale = gate_column_magnitude / jnp.sqrt(gate_sq + stability_offset)
    up_column_scale = up_column_magnitude / jnp.sqrt(up_sq + stability_offset)
    down_column_scale = down_column_magnitude / jnp.sqrt(down_squared + stability_offset)
    gate_coordinate_slice = jnp.dot(
        token_rows_full, gate_left_factor, preferred_element_type=jnp.float32
    )
    up_coordinate_slice = jnp.dot(
        token_rows_full, up_left_factor, preferred_element_type=jnp.float32
    )
    local_gate_slice, local_up_slice = tuple(
        (
            part.astype(jnp.float32)
            for part in sent_together(
                (
                    gate_coordinate_slice.astype(jnp.bfloat16),
                    up_coordinate_slice.astype(jnp.bfloat16),
                ),
                "col",
                0,
                1,
            )
        )
    )
    summed = lax.psum_scatter(
        jnp.concatenate(
            [
                plain_term(token_rows_full, gate_frozen_weight),
                plain_term(token_rows_full, up_frozen_weight),
            ],
            axis=1,
        ).astype(jnp.bfloat16),
        "col",
        scatter_dimension=0,
        tiled=True,
    ).astype(jnp.float32)
    split_at = gate_frozen_weight.shape[1]
    gate_total = summed[:, :split_at]
    up_total = summed[:, split_at:]
    gate_total = gate_total + jnp.dot(
        local_gate_slice, gate_right_factor.astype(jnp.float32), precision=lax.Precision.HIGHEST
    )
    up_total = up_total + jnp.dot(
        local_up_slice, up_right_factor.astype(jnp.float32), precision=lax.Precision.HIGHEST
    )
    hidden_values = (
        jax.nn.silu(gate_total * gate_column_scale[None, :]) * (up_total * up_column_scale[None, :])
    ).astype(jnp.bfloat16)
    hidden_full = lax.all_gather(hidden_values, "col", axis=0, tiled=True)
    mixed = sum_at_owner(
        rank_update_term(
            hidden_full, down_frozen_weight, down_left_factor, down_right_factor
        ).astype(jnp.bfloat16),
        "row",
        0,
    )
    return (mixed * down_column_scale[None, :]).astype(jnp.bfloat16)


def solution(mesh):
    placed = (
        P("row", "col"),
        P("col", "row"),
        P("col", None),
        P(None, "row"),
        P("row"),
        P("col", "row"),
        P("col", None),
        P(None, "row"),
        P("row"),
        P("row", "col"),
        P("row", None),
        P(None, "col"),
        P("col"),
    )
    return jax.shard_map(
        shards, mesh=mesh, in_specs=placed, out_specs=P("row", "col"), check_vma=False
    )
```

profile of v0, /device:TPU:0, one launch (start us, length us, event | category | flops | bytes accessed | tf_op | source)
XLA Modules:
  0.0 529.3 jit_solution(13514375296845573576)
XLA Ops:
  6.5 0.0 reduce-scatter.5.cloned.1.call-start
  6.5 1.3 broadcast_in_dim.12
  7.8 33.5 %all_to_all.22 = bf16[8,256,512]{2,1,0:T(8,128)(2,1)S(1)} all-to-all(bf16[8,256,512]{2,1,0:T(8,128)(2,1)S(1)} %broadcast_in_dim.12), channel_id=1, replica_groups=mesh['row'=8,'col'=16] {'row'}, dimensions={0} | all-to-all | bytes 4194304 | tf_op jit(solution)/shard_map/all_to_all | solution.py:17
  41.4 11.0 %convolution_convert_fusion = bf16[2048,3584]{1,0:T(8,128)(2,1)} fusion(bf16[2048,512]{1,0:T(8,128)(2,1)S(1)} %bitcast.25, bf16[512,3584]{1,0:T(8,128)(2,1)S(1)} %copy-done.12), kind=kOutput, calls=%fused_computation.1 | convolution fusion | flops 7523532800 | bytes 20447232 | tf_op jit(solution)/shard_map/dot_general | solution.py:63
  52.3 0.0 copy-done.11
  52.3 11.0 %convolution_convert_fusion.1 = bf16[2048,3584]{1,0:T(8,128)(2,1)} fusion(bf16[2048,512]{1,0:T(8,128)(2,1)S(1)} %bitcast.26, bf16[512,3584]{1,0:T(8,128)(2,1)S(1)} %copy-done.11), kind=kOutput, calls=%fused_computation.2 | convolution fusion | flops 7523532800 | bytes 20447232 | tf_op jit(solution)/shard_map/dot_general | solution.py:63
  63.3 20.2 %pad_maximum_fusion = bf16[2048,7168]{1,0:T(8,128)(2,1)} fusion(bf16[2048,3584]{1,0:T(8,128)(2,1)} %convolution_convert_fusion, bf16[2048,3584]{1,0:T(8,128)(2,1)} %convolution_convert_fusion.1), kind=kLoop, calls=%fused_computation | loop fusion | flops 58720256 | bytes 58720256 | tf_op jit(solution)/shard_map/concatenate | solution.py:122
  83.5 0.0 copy-start.5
  83.5 0.0 reduce-scatter.5.cloned.1.call-update
  83.5 0.0 copy-start.6
  83.5 0.0 reduce-scatter.7.cloned.1.call-start
  83.6 0.0 copy-done
  83.6 0.7 copy-done.5
  84.3 3.2 multiply_reduce_fusion.2
  87.5 0.0 copy-start.14
  87.6 0.8 convolution_convert_fusion.3
  88.3 0.7 convolution_convert_fusion.2
  89.1 1.0 copy.16
  90.1 0.0 reduce-scatter.7.cloned.1.call-update
  90.2 0.0 copy-start.8
  90.2 0.0 copy-start.9
  90.2 0.0 all-gather.2.cloned.1.call-start
  90.2 0.0 copy-done.14
  90.2 4.3 multiply_reduce_fusion.1
  94.5 0.2 broadcast_in_dim.13
  94.8 18.2 %all_to_all.23 = f32[16,1,7168]{2,1,0:T(1,128)S(1)} all-to-all(f32[16,1,7168]{2,1,0:T(1,128)S(1)} %broadcast_in_dim.13), channel_id=1, replica_groups=mesh['row'=8,'col'=16] {'col'}, dimensions={0} | all-to-all | bytes 917504 | tf_op jit(solution)/shard_map/all_to_all | solution.py:17
  113.0 0.3 reduce_sum.56
  113.3 184.8 %reduce-scatter.5.cloned.1.call-done = bf16[128,7168]{1,0:T(8,128)(2,1)} async-done(((bf16[2048,7168]{1,0:T(8,128)(2,1)}), bf16[128,7168]{1,0:T(8,128)(2,1)}) %reduce-scatter.5.cloned.1.call-update) | async-done | bytes 1835024 | tf_op jit(solution)/shard_map/reduce_scatter | solution.py:121
  298.1 3.7 convert_element_type.36
  301.7 63.6 %reduce-scatter.7.cloned.1.call-done = bf16[128,128]{1,0:T(8,128)(2,1)} async-done(((bf16[2048,128]{1,0:T(8,128)(2,1)}), bf16[128,128]{1,0:T(8,128)(2,1)}) %reduce-scatter.7.cloned.1.call-update) | async-done | bytes 32784
  365.3 2.0 fusion.2
  367.4 0.5 copy-done.2
  367.9 1.7 fusion.3
  369.6 0.0 all-gather.2.cloned.1.call-update
  369.7 3.2 multiply_reduce_fusion
  372.9 0.6 broadcast_in_dim.14
  373.5 4.8 all-to-all-start.3
  378.3 89.9 %all-gather.2.cloned.1.call-done = bf16[2048,3584]{1,0:T(8,128)(2,1)} async-done(((bf16[128,3584]{1,0:T(8,128)(2,1)}), bf16[2048,3584]{1,0:T(8,128)(2,1)}) %all-gather.2.cloned.1.call-update) | async-done | bytes 14680080 | tf_op jit(solution)/shard_map/all_gather | solution.py:145
  468.2 9.8 %fusion.11 = f32[2048,64]{0,1:T(8,128)S(1)} fusion(bf16[2048,3584]{1,0:T(8,128)(2,1)} %all-gather.2.cloned.1.call-done, bf16[3584,64]{0,1:T(8,128)(2,1)S(1)} %copy-done.3), kind=kOutput, calls=%fused_computation.29 | convolution fusion | flops 939524096 | bytes 15663104 | tf_op jit(solution)/shard_map/dot_general | solution.py:68
  478.0 0.0 copy-done.1
  478.0 0.6 copy-done.13
  478.5 7.8 %fusion.10 = f32[2048,512]{1,0:T(8,128)S(1)} fusion(bf16[2048,3584]{1,0:T(8,128)(2,1)S(1)} %copy-done.1, bf16[3584,512]{1,0:T(8,128)(2,1)S(1)} %copy-done.13), kind=kOutput, calls=%fused_computation.28 | convolution fusion | flops 7516192768 | bytes 22544384 | tf_op jit(solution)/shard_map/dot_general | solution.py:67
  486.3 3.4 add_convert_fusion
  489.7 0.0 all-to-all-done.3
  489.7 4.6 all-to-all-start.2
  494.3 27.3 %all-to-all-done.2 = bf16[8,256,512]{2,1,0:T(8,128)(2,1)S(1)} async-done(((bf16[8,256,512]{2,1,0:T(8,128)(2,1)}), bf16[8,256,512]{2,1,0:T(8,128)(2,1)S(1)}, u32[]{:S(2)}, u32[]{:S(2)}) %all-to-all-start.2) | async-done | bytes 2097184 | tf_op jit(solution)/shard_map/all_to_all | solution.py:53
  521.7 0.3 convert_reduce_fusion
  522.0 0.7 multiply_convert_fusion
  (23 shorter events, 0.1 us)
Async XLA Ops:
  6.5 77.0 %copy-start = (bf16[64,3584]{1,0:T(8,128)(2,1)S(1)}, bf16[64,3584]{1,0:T(8,128)(2,1)}, u32[]{:S(2)}) copy-start(bf16[64,3584]{1,0:T(8,128)(2,1)} %param.16) | copy-start | bytes 1376260
  6.5 291.5 %reduce-scatter.5.cloned.1.call-start = ((), (), s32[]{:S(2)}) async-start(), calls=%async_computation.6 | async-start | bytes 31195136 | tf_op jit(solution)/shard_map/reduce_scatter | solution.py:121
  6.5 34.8 %copy-start.12 = (bf16[512,3584]{1,0:T(8,128)(2,1)S(1)}, bf16[512,3584]{1,0:T(8,128)(2,1)}, u32[]{:S(2)}) copy-start(bf16[512,3584]{1,0:T(8,128)(2,1)} %param.18) | copy-start | bytes 11010052
  41.3 11.0 %copy-start.11 = (bf16[512,3584]{1,0:T(8,128)(2,1)S(1)}, bf16[512,3584]{1,0:T(8,128)(2,1)}, u32[]{:S(2)}) copy-start(bf16[512,3584]{1,0:T(8,128)(2,1)} %param.14) | copy-start | bytes 11010052
  83.5 0.8 copy-start.5
  83.5 4.8 copy-start.6
  83.5 281.8 %reduce-scatter.7.cloned.1.call-start = ((), (), s32[]{:S(2)}) async-start(), calls=%async_computation.8 | async-start | bytes 557056
  87.5 2.7 copy-start.14
  90.2 23.1 %copy-start.8 = (f32[3584]{0:T(1024)S(1)}, f32[3584]{0:T(1024)}, u32[]{:S(2)}) copy-start(f32[3584]{0:T(1024)} %param.21) | copy-start | bytes 43012
  90.2 23.1 %copy-start.9 = (f32[3584]{0:T(1024)S(1)}, f32[3584]{0:T(1024)}, u32[]{:S(2)}) copy-start(f32[3584]{0:T(1024)} %param.17) | copy-start | bytes 43012
  90.2 378.0 %all-gather.2.cloned.1.call-start = ((), (), s32[]{:S(2)}) async-start(), calls=%async_computation.7 | async-start | bytes 15597568 | tf_op jit(solution)/shard_map/all_gather | solution.py:145
  365.3 2.6 copy-start.2
  365.3 2.6 copy-start.7
  367.9 1.7 copy-start.3
  367.9 1.7 copy-start.4
  373.5 116.2 %all-to-all-start.3 = ((f32[8,1,512]{2,1,0:T(1,128)}), f32[8,1,512]{2,1,0:T(1,128)S(1)}, u32[]{:S(2)}, u32[]{:S(2)}) async-start(f32[8,1,512]{2,1,0:T(1,128)} %broadcast_in_dim.14), calls=%async_computation.4 | async-start | bytes 32768 | tf_op jit(solution)/shard_map/all_to_all | solution.py:17
  468.1 9.8 %copy-start.1 = (bf16[2048,3584]{1,0:T(8,128)(2,1)S(1)}, bf16[2048,3584]{1,0:T(8,128)(2,1)}, u32[]{:S(2)}) copy-start(bf16[2048,3584]{1,0:T(8,128)(2,1)} %all-gather.2.cloned.1.call-done) | copy-start | bytes 44040196
  468.1 10.4 %copy-start.13 = (bf16[3584,512]{1,0:T(8,128)(2,1)S(1)}, bf16[3584,512]{1,0:T(8,128)(2,1)}, u32[]{:S(2)}) copy-start(bf16[3584,512]{1,0:T(8,128)(2,1)} %param.22) | copy-start | bytes 11010052
  489.7 4.6 copy-start.10
  489.7 32.0 %all-to-all-start.2 = ((bf16[8,256,512]{2,1,0:T(8,128)(2,1)}), bf16[8,256,512]{2,1,0:T(8,128)(2,1)S(1)}, u32[]{:S(2)}, u32[]{:S(2)}) async-start(bf16[8,256,512]{2,1,0:T(8,128)(2,1)} %bitcast.29), calls=%async_computation.3 | async-start | bytes 4194304 | tf_op jit(solution)/shard_map/all_to_all | solution.py:53
Sparse Core Ops, SparseCore 0:
  83.6 214.3 reduce-scatter.4
  301.8 63.5 reduce-scatter.6
  369.8 98.3 all-gather.1
where the time goes:
time: 530 us; the launch traced here: 529 us
  waiting for transfers between devices  366 us (69%)
  matrix products  58.8 us (11%)
  blocking collectives  51.7 us (10%)
  other arithmetic  25.3 us (5%)
  between operations  13.3 us (3%)
  starting transfers between devices  9.42 us (2%)
    reduce_scatter x1, waiting for transfers between devices, shards(): lax.psum_scatter(jnp.concatenate([plain_term(token_rows_full, gate_frozen...  185 us
    all_gather x1, waiting for transfers between devices, shards(): hidden_full = lax.all_gather(hidden_values, 'col', axis=0, tiled=True)  89.9 us
    unnamed x4, waiting for transfers between devices  63.7 us
    all_to_all x2, blocking collectives, from_everyone(): return lax.all_to_all(copies, axis, split_axis=0, concat_axis=0, tiled=True)  51.7 us
    all_to_all x1, waiting for transfers between devices, sum_at_owner(): tiles = lax.all_to_all(cut_along(value, dim, size), axis, 0, 0, tiled=True)  27.3 us
    dot_general x2, matrix products, plain_term(): return jnp.dot(inputs, weight, preferred_element_type=jnp.float32)  21.9 us
    concatenate x1, other arithmetic, shards(): jnp.concatenate([plain_term(token_rows_full, gate_frozen_weight), plain_t...  20.2 us
    dot_general x3, matrix products, column_square_totals(): jnp.dot(low_b, low_a, preferred_element_type=jnp.float32)  10.7 us
  transfers between devices with their start and end apart: 5, of which 4 were waited for; matrix products, arithmetic and copies ran while one was open for 7% of the time, Pallas kernels for 0%

commit v1 on v0

v1 whole, which is shorter than its diff:
```python
import functools

import jax
import jax.numpy as jnp
from jax import lax
from jax.experimental import pallas as pl
from jax.experimental.pallas import tpu as pltpu
from jax.sharding import PartitionSpec as P

stability_offset = 1e-06
MESH = pl.DeviceIdType.MESH
NJ = 7


def place():
    r = lax.axis_index("row")
    c = lax.axis_index("col")
    return r // 2, r % 2, c // 4, (c // 2) % 2, c % 2


def device(z, xlo, y, xhi, core):
    return (z * 2 + xlo, (y * 2 + xhi) * 2 + core)


def greet(peers):
    barrier = pltpu.get_barrier_semaphore()
    for peer in peers:
        pl.semaphore_signal(barrier, inc=1, device_id=peer, device_id_type=MESH)
    pl.semaphore_wait(barrier, len(peers))


def send(src, dst, ss, rs, peer):
    return pltpu.make_async_remote_copy(
        src_ref=src, dst_ref=dst, send_sem=ss, recv_sem=rs, device_id=peer, device_id_type=MESH
    )


def column_scale(magnitude, squares):
    return magnitude / jnp.sqrt(squares + stability_offset)


def hidden_kernel(
    tok, gate_w, up_w, left, gate_r, up_r, gate_m, up_m, hid,
    X, W, L, A_s, B_s, C_s, A_r, B_r, C_r, q_s, q_r,
    own, xs, xr, zs, zr, fs, fr, ds, dr, wl, ws, wr, ls, lr, as_, ar, bs, br, cs, cr, qs, qr,
):
    z, xlo, y, xhi, core = place()
    x = xhi * 2 + xlo
    q = xhi * 2 + core
    rb = z * 2 + xlo

    def at_x(d):
        n = (x + d) % 4
        return device(z, n % 2, y, n // 2, core)

    def at_z(d):
        return device((z + d) % 4, xlo, y, xhi, core)

    def at_y(d):
        return device(z, xlo, (y + d) % 4, xhi, core)

    mate = device(z, xlo, y, xhi, 1 - core)
    group = (mate, device(z, xlo, y, 1 - xhi, core), device(z, xlo, y, 1 - xhi, 1 - core))
    group_q = (xhi * 2 + 1 - core, (1 - xhi) * 2 + core, (1 - xhi) * 2 + 1 - core)
    greet((
        at_x(1), at_x(2), at_x(3), at_z(1), at_z(3), mate, group[2], at_y(1), at_y(2), at_y(3),
    ))

    def tile(dz, d, lo=0, n=256):
        xt = (x + 4 - d) % 4
        zt = (z + dz) % 4
        lane = pl.multiple_of(((xt // 2) * 2 + core) * 512, 512)
        return X.at[zt * 2 + xt % 2, pl.ds(lo, n), pl.ds(lane, 512)]

    mine = tile(0, 0)
    started = []

    def go(copy):
        copy.start()
        started.append(copy)
        return copy

    x_in = [None] * 4
    for d in (1, 3, 2):
        x_in[d] = go(send(tok, mine, xs.at[d - 1], xr.at[d - 1], at_x(d)))
    z_in = [[None] * 4, [None] * 4]
    z_in[0][0] = go(send(tok, mine, zs.at[0, 0], zr.at[0, 0], at_z(1)))
    z_in[1][0] = go(send(tok, mine, zs.at[1, 0], zr.at[1, 0], at_z(3)))
    d_in = [[None] * 4 for _ in range(4)]
    d_in[0][0] = go(send(tok, mine, ds.at[0, 0], dr.at[0, 0], mate))
    keep = pltpu.make_async_copy(tok, mine, own.at[0])
    keep.start()

    rows = pl.ds(pl.multiple_of(q * 512, 512), 512)
    l_in = [go(send(left, L.at[rows], ls.at[t], lr.at[t], group[t])) for t in range(3)]
    keep_l = pltpu.make_async_copy(left, L.at[rows], own.at[1])
    keep_l.start()

    def weight_copies(j):
        local, remote = [], []
        for g, w in enumerate((gate_w, up_w)):
            dst = W.at[j, rows, pl.ds(g * 128, 128)]
            for t in (1, 2, 0):
                cols = pl.ds(pl.multiple_of(group_q[t] * 896 + j * 128, 128), 128)
                remote.append(send(w.at[:, cols], dst, ws.at[j, g, t], wr.at[j, g, t], group[t]))
            cols = pl.ds(pl.multiple_of(q * 896 + j * 128, 128), 128)
            local.append(pltpu.make_async_copy(w.at[:, cols], dst, wl.at[j, g]))
        return local, remote

    def fetch(j):
        local, remote = weight_copies(j)
        for copy in remote + local:
            copy.start()

    fetch(0)

    for d in (1, 3, 2):
        x_in[d].wait_recv()
        here = tile(0, d)
        z_in[0][d] = go(send(here, here, zs.at[0, d], zr.at[0, d], at_z(1)))
        z_in[1][d] = go(send(here, here, zs.at[1, d], zr.at[1, d], at_z(3)))
        d_in[0][d] = go(send(here, here, ds.at[0, d], dr.at[0, d], mate))
    fetch(1)
    f_in = [[None] * 4, [None] * 4]
    for d in (0, 1, 3, 2):
        for s in range(2):
            z_in[s][d].wait_recv()
            dz = 3 if s == 0 else 1
            part = tile(dz, d, 128 * s, 128)
            f_in[s][d] = go(send(part, part, fs.at[s, d], fr.at[s, d], at_z(1 if s == 0 else 3)))
            here = tile(dz, d)
            d_in[1 + s][d] = go(send(here, here, ds.at[1 + s, d], dr.at[1 + s, d], mate))
        if d in (0, 1, 3):
            fetch((2, 3, None, 4)[d])
    for d in (0, 1, 3, 2):
        f_in[0][d].wait_recv()
        f_in[1][d].wait_recv()
        here = tile(2, d)
        d_in[3][d] = go(send(here, here, ds.at[3, d], dr.at[3, d], mate))
    keep.wait()
    keep_l.wait()
    for copy in l_in:
        copy.wait_recv()
    for i in range(4):
        for d in range(4):
            d_in[i][d].wait_recv()

    def partial(b, h, j):
        t = X[pl.ds(4 * h, 4), pl.ds(pl.multiple_of(b * 64, 64), 64), :].reshape(256, 2048)
        return jnp.dot(t, W[j], preferred_element_type=jnp.float32)

    def chain(j, h):
        return send(A_s.at[j, h], A_r.at[j, h], as_.at[j, h], ar.at[j, h], at_y(1 if h == 0 else 3))

    def direct(j, h):
        return send(B_s.at[j, h], B_r.at[j, h], bs.at[j, h], br.at[j, h], at_y(3 if h == 0 else 1))

    def last(j, h):
        return send(C_s.at[j, h], C_r.at[j, h], cs.at[j, h], cr.at[j, h], at_y(1 if h == 0 else 3))

    def squares(j):
        return [send(q_s.at[j], q_r.at[j, d - 1], qs.at[j, d - 1], qr.at[j, d - 1], at_y(d)) for d in (1, 2, 3)]

    def finish(j):
        for copy in squares(j):
            copy.wait_recv()
        sq = jnp.sum(q_s[j] + q_r[j, 0] + q_r[j, 1] + q_r[j, 2], axis=0, keepdims=True)
        cols = pl.ds(pl.multiple_of(q * 896 + j * 128, 128), 128)
        gate_scale = column_scale(gate_m[:, cols], sq[:, :128])
        up_scale = column_scale(up_m[:, cols], sq[:, 128:])
        for h in range(2):
            direct(j, h).wait_recv()
            last(j, h).wait_recv()
            total = partial(y, h, j) + B_r[j, h].astype(jnp.float32) + C_r[j, h].astype(jnp.float32)
            gate = total[:, :128] * gate_scale
            up = total[:, 128:] * up_scale
            value = gate / (1.0 + jnp.exp(-gate)) * up
            hid[pl.ds(4 * h, 4), :, pl.ds(pl.multiple_of(j * 128, 128), 128)] = value.astype(
                jnp.bfloat16
            ).reshape(4, 64, 128)

    @pl.loop(0, NJ)
    def _(j):
        @pl.when(j < NJ - 5)
        def _():
            fetch(j + 5)

        local, remote = weight_copies(j)
        for copy in local:
            copy.wait()
        for copy in remote:
            copy.wait_recv()
        cols = pl.ds(pl.multiple_of(q * 896 + j * 128, 128), 128)
        zero = jnp.zeros((64, 128), jnp.bfloat16)
        right = jnp.concatenate(
            [
                jnp.concatenate([gate_r[:, cols], zero], axis=1),
                jnp.concatenate([zero, up_r[:, cols]], axis=1),
            ],
            axis=0,
        )
        q_s[j] = jnp.zeros((8, 256), jnp.float32)

        @pl.loop(0, 8)
        def _(i):
            part = pl.ds(pl.multiple_of(i * 256, 256), 256)
            merged = W[j, part].astype(jnp.float32) + jnp.dot(
                L[part], right, preferred_element_type=jnp.float32
            )
            q_s[j] += jnp.sum((merged * merged).reshape(32, 8, 256), axis=0)
            W[j, part] = merged.astype(jnp.bfloat16)

        for h in range(2):
            A_s[j, h] = partial((y + 2) % 4, h, j).astype(jnp.bfloat16)
            chain(j, h).start()
        for copy in squares(j):
            copy.start()
        for h in range(2):
            B_s[j, h] = partial((y + (3 if h == 0 else 1)) % 4, h, j).astype(jnp.bfloat16)
            direct(j, h).start()
        for h in range(2):
            value = partial((y + (1 if h == 0 else 3)) % 4, h, j)
            chain(j, h).wait_recv()
            C_s[j, h] = (value + A_r[j, h].astype(jnp.float32)).astype(jnp.bfloat16)
            last(j, h).start()

        @pl.when(j >= 1)
        def _():
            finish(j - 1)

    finish(NJ - 1)

    for copy in started:
        copy.wait_send()

    @pl.loop(0, NJ)
    def _(j):
        for copy in weight_copies(j)[1] + squares(j):
            copy.wait_send()
        for h in range(2):
            chain(j, h).wait_send()
            direct(j, h).wait_send()
            last(j, h).wait_send()


def hidden_of(tok, gate_w, up_w, left, gate_r, up_r, gate_m, up_m):
    anywhere = pl.BlockSpec(memory_space=pl.ANY)
    vmem = pl.BlockSpec(memory_space=pltpu.VMEM)
    dma = lambda *s: pltpu.SemaphoreType.DMA(s)
    piece = lambda: pltpu.VMEM((NJ, 2, 256, 256), jnp.bfloat16)
    return pl.pallas_call(
        hidden_kernel,
        out_shape=jax.ShapeDtypeStruct((8, 64, 896), jnp.bfloat16),
        in_specs=[anywhere, anywhere, anywhere, vmem, vmem, vmem, vmem, vmem],
        out_specs=vmem,
        scratch_shapes=[
            pltpu.VMEM((8, 256, 2048), jnp.bfloat16),
            pltpu.VMEM((NJ, 2048, 256), jnp.bfloat16),
            pltpu.VMEM((2048, 128), jnp.bfloat16),
            piece(), piece(), piece(), piece(), piece(), piece(),
            pltpu.VMEM((NJ, 8, 256), jnp.float32),
            pltpu.VMEM((NJ, 3, 8, 256), jnp.float32),
            dma(2), dma(3), dma(3), dma(2, 4), dma(2, 4), dma(2, 4), dma(2, 4), dma(4, 4), dma(4, 4),
            dma(NJ, 2), dma(NJ, 2, 3), dma(NJ, 2, 3), dma(3), dma(3),
            dma(NJ, 2), dma(NJ, 2), dma(NJ, 2), dma(NJ, 2), dma(NJ, 2), dma(NJ, 2),
            dma(NJ, 3), dma(NJ, 3),
        ],
        compiler_params=pltpu.CompilerParams(
            collective_id=0, has_side_effects=True, vmem_limit_bytes=60 * 2**20
        ),
        name="hidden_kernel",
    )(tok, gate_w, up_w, left, gate_r, up_r, gate_m, up_m)


def shards(
    tokens,
    gate_frozen_weight, gate_left_factor, gate_right_factor, gate_column_magnitude,
    up_frozen_weight, up_left_factor, up_right_factor, up_column_magnitude,
    down_frozen_weight, down_left_factor, down_right_factor, down_column_magnitude,
):
    left = jnp.concatenate([gate_left_factor, up_left_factor], axis=1)
    hidden = hidden_of(
        tokens, gate_frozen_weight, up_frozen_weight, left, gate_right_factor, up_right_factor,
        gate_column_magnitude[None], up_column_magnitude[None],
    )
    merged = down_frozen_weight.astype(jnp.float32) + jnp.dot(
        down_left_factor, down_right_factor, preferred_element_type=jnp.float32
    )
    squares = jnp.sum(merged * merged, axis=0)
    squares = lax.psum(squares, "row")
    scale = column_scale(down_column_magnitude, squares)
    full = lax.all_gather(hidden, "col", axis=0, tiled=False)
    full = full.reshape(4, 4, 8, 64, 896).transpose(2, 0, 3, 1, 4).reshape(2048, 3584)
    out = jnp.dot(full, merged.astype(jnp.bfloat16), preferred_element_type=jnp.float32)
    tiles = lax.all_to_all(out.astype(jnp.bfloat16).reshape(8, 256, 512), "row", 0, 0, tiled=True)
    mixed = jnp.sum(tiles.astype(jnp.float32), axis=0)
    return (mixed * scale[None, :]).astype(jnp.bfloat16)


def solution(mesh):
    placed = (
        P("row", "col"),
        P("col", "row"), P("col", None), P(None, "row"), P("row"),
        P("col", "row"), P("col", None), P(None, "row"), P("row"),
        P("row", "col"), P("row", None), P(None, "col"), P("col"),
    )
    return jax.shard_map(
        shards, mesh=mesh, in_specs=placed, out_specs=P("row", "col"), check_vma=False
    )
```

time: 530 us -> 396 us (0.75)
  waiting for transfers between devices: 366 us -> 92.2 us
  Pallas kernels: 0 us -> 201 us
  matrix products: 58.8 us -> 17.1 us
  local copies, waits for them, and re-layouts: 5.04 us -> 28.8 us
  other arithmetic: 25.3 us -> 1.81 us
  blocking collectives: 51.7 us -> 37.2 us
    pallas_call x0 -> x1, Pallas kernels: none -> 201 us  [hidden_of(): pl.pallas_call(hidden_kernel, out_shape=jax.ShapeDtypeStruct((8, 64, 896)...]
    reduce_scatter x1 -> x0, waiting for transfers between devices: 185 us -> none  [shards(): lax.psum_scatter(jnp.concatenate([plain_term(token_rows_full, gate_frozen...]
    unnamed x4 -> x1, waiting for transfers between devices: 63.7 us -> 0.02 us
    all_to_all x2 -> x0, blocking collectives: 51.7 us -> none  [from_everyone(): return lax.all_to_all(copies, axis, split_axis=0, concat_axis=0, tiled=True)]
    dot_general x12 -> x2, matrix products: 58.8 us -> 17.1 us  [the longest x1 12 us: shards(): jnp.dot(full, merged.astype(jnp.bfloat16), preferred_element_type=jnp.flo...]
    psum x0 -> x1, blocking collectives: none -> 37.2 us  [shards(): squares = lax.psum(squares, 'row')]
    all_to_all x2 -> x1, waiting for transfers between devices: 27.3 us -> 0.01 us  [shards(): lax.all_to_all(out.astype(jnp.bfloat16).reshape(8, 256, 512), 'row', 0, 0...]
    concatenate x3 -> x1, other arithmetic: 20.3 us -> 0.77 us  [shards(): left = jnp.concatenate([gate_left_factor, up_left_factor], axis=1)]
  transfers between devices with their start and end apart: 5 -> 2, of which waited for: 4 -> 1; matrix products, arithmetic and copies ran while one was open for 7% -> 1% of each run, Pallas kernels for 0% -> 0%
where the time goes in v1:
time: 396 us
  Pallas kernels  201 us (51%)
  waiting for transfers between devices  92.2 us (23%)
  blocking collectives  37.2 us (9%)
  local copies, waits for them, and re-layouts  28.8 us (7%)
  matrix products  17.1 us (4%)
  between operations  13.5 us (3%)
  starting transfers between devices  4.57 us (1%)
    pallas_call x1, Pallas kernels, hidden_of(): pl.pallas_call(hidden_kernel, out_shape=jax.ShapeDtypeStruct((8, 64, 896)...  201 us
    all_gather x1, waiting for transfers between devices, shards(): full = lax.all_gather(hidden, 'col', axis=0, tiled=False)  92.2 us
    psum x1, blocking collectives, shards(): squares = lax.psum(squares, 'row')  37.2 us
    reshape x1, local copies, waits for them, and re-layouts, shards(): full.reshape(4, 4, 8, 64, 896).transpose(2, 0, 3, 1, 4).reshape(2048, 3584)  16.9 us
    dot_general x1, matrix products, shards(): jnp.dot(full, merged.astype(jnp.bfloat16), preferred_element_type=jnp.flo...  12 us
    unnamed x11, local copies, waits for them, and re-layouts  9.2 us
  transfers between devices with their start and end apart: 2, of which 1 were waited for; matrix products, arithmetic and copies ran while one was open for 1% of the time, Pallas kernels for 0%

profile of v1, /device:TPU:0, one launch (start us, length us, event | category | flops | bytes accessed | tf_op | source)
XLA Modules:
  0.0 395.8 jit_solution(9463804310690773808)
XLA Ops:
  6.5 0.0 copy-start
  6.5 0.0 all-gather.3.cloned.1.call-start
  6.5 1.4 broadcast_in_dim.7.gate_m
  7.9 1.3 broadcast_in_dim.8.up_m
  9.2 1.0 copy.19
  10.2 1.0 copy.20
  11.2 0.8 pad_maximum_fusion.left
  11.9 0.0 copy-start.2
  11.9 200.6 %hidden_kernel.1 = bf16[8,64,896]{2,1,0:T(8,128)(2,1)} custom-call(bf16[256,512]{1,0:T(8,128)(2,1)} %tok.1, bf16[512,3584]{1,0:T(8,128)(2,1)} %gate_w.1, bf16[512,3584]{1,0:T(8,128)(2,1)} %up_w.1, bf16[512,128]{1,0:T(8,128)(2,1)} %pad_maximum_fusion.left, bf16[64,3584]{1,0:T(8,128)(2,1)} %gate_r.1, bf16[64,3584]{1,0:T(8,128)(2,1)} %up_r.1, ...), custom_call_target="tpu_custom_call" | custom-call | tf_op jit(solution)/shard_map/hidden_kernel/pallas_call | solution.py:251
  212.6 0.0 all-gather.3.cloned.1.call-update
  212.6 0.0 copy-done
  212.6 0.0 copy-done.2
  212.6 5.1 %multiply_reduce_fusion = (f32[512]{0:T(512)S(1)}, bf16[3584,512]{1,0:T(8,128)(2,1)}) fusion(bf16[3584,64]{0,1:T(8,128)(2,1)S(1)} %copy-done, bf16[64,512]{1,0:T(8,128)(2,1)S(1)} %copy-done.2, bf16[3584,512]{1,0:T(8,128)(2,1)} %param.22), kind=kOutput, calls=%fused_computation | convolution fusion | flops 244055552 | bytes 7866368 | tf_op jit(solution)/shard_map/dot_general | solution.py:286
  217.7 92.2 %all-gather.3.cloned.1.call-done = bf16[128,64,896]{2,1,0:T(8,128)(2,1)} async-done(((bf16[8,64,896]{2,1,0:T(8,128)(2,1)}), bf16[128,64,896]{2,1,0:T(8,128)(2,1)}) %all-gather.3.cloned.1.call-update) | async-done | bytes 14680080 | tf_op jit(solution)/shard_map/all_gather | solution.py:292
  309.9 16.9 %copy.21 = bf16[4,4,8,64,896]{4,1,3,0,2:T(4,128)(2,1)S(1)} copy(bf16[4,4,8,64,896]{4,3,2,1,0:T(8,128)(2,1)} %bitcast.11) | data formatting | bytes 29360128 | tf_op jit(solution)/shard_map/reshape | solution.py:293
  326.9 0.0 copy-start.3
  326.9 7.3 %copy.22 = bf16[256,8,4,896]{3,1,2,0:T(8,128)(2,1)} copy(bf16[256,8,4,896]{3,2,1,0:T(4,128)(2,1)S(1)} %bitcast.10) | data formatting | bytes 29360128
  334.2 0.0 copy-done.3
  334.2 12.0 %fusion.2 = bf16[2048,512]{1,0:T(8,128)(2,1)} fusion(bf16[2048,3584]{1,0:T(8,128)(2,1)} %bitcast.12, bf16[3584,512]{1,0:T(8,128)(2,1)S(1)} %copy-done.3), kind=kOutput, calls=%fused_computation.5 | convolution fusion | flops 7517241344 | bytes 20447232 | tf_op jit(solution)/shard_map/dot_general | solution.py:294
  346.1 0.0 copy-start.1
  346.1 4.6 %all-to-all-start = ((bf16[8,256,512]{2,1,0:T(8,128)(2,1)}), bf16[8,256,512]{2,1,0:T(8,128)(2,1)S(1)}, u32[]{:S(2)}, u32[]{:S(2)}) async-start(bf16[8,256,512]{2,1,0:T(8,128)(2,1)} %bitcast.13), calls=%async_computation | async-start | bytes 4194304 | tf_op jit(solution)/shard_map/all_to_all | solution.py:295
  350.7 37.2 %psum.7 = f32[512]{0:T(512)S(1)} all-reduce(f32[512]{0:T(512)S(1)} %get-tuple-element.5), channel_id=1, replica_groups=mesh['row'=8,'col'=16] {'row'}, use_global_device_ids=true, to_apply=%region_2.0 | all-reduce | flops 512 | bytes 4096 | tf_op jit(solution)/shard_map/psum | solution.py:290
  387.9 0.0 copy-done.1
  387.9 0.0 all-to-all-done
  387.9 0.3 convert_reduce_fusion
  388.2 0.7 multiply_convert_fusion
  (1 shorter events, 0.0 us)
Async XLA Ops:
  6.5 206.1 %copy-start = (bf16[3584,64]{0,1:T(8,128)(2,1)S(1)}, bf16[3584,64]{0,1:T(8,128)(2,1)}, u32[]{:S(2)}) copy-start(bf16[3584,64]{0,1:T(8,128)(2,1)} %param.23) | copy-start | bytes 1376260
  6.5 303.4 %all-gather.3.cloned.1.call-start = ((), (), s32[]{:S(2)}) async-start(), calls=%async_computation.1 | async-start | bytes 15597568 | tf_op jit(solution)/shard_map/all_gather | solution.py:292
  11.9 200.7 %copy-start.2 = (bf16[64,512]{1,0:T(8,128)(2,1)S(1)}, bf16[64,512]{1,0:T(8,128)(2,1)}, u32[]{:S(2)}) copy-start(bf16[64,512]{1,0:T(8,128)(2,1)} %param.24) | copy-start | bytes 196612
  326.9 7.3 %copy-start.3 = (bf16[3584,512]{1,0:T(8,128)(2,1)S(1)}, bf16[3584,512]{1,0:T(8,128)(2,1)}, u32[]{:S(2)}) copy-start(bf16[3584,512]{1,0:T(8,128)(2,1)} %get-tuple-element.6) | copy-start | bytes 11010052
  346.1 41.7 %copy-start.1 = (f32[512]{0:T(512)S(1)}, f32[512]{0:T(512)}, u32[]{:S(2)}) copy-start(f32[512]{0:T(512)} %param.25) | copy-start | bytes 6148
  346.1 41.8 %all-to-all-start = ((bf16[8,256,512]{2,1,0:T(8,128)(2,1)}), bf16[8,256,512]{2,1,0:T(8,128)(2,1)S(1)}, u32[]{:S(2)}, u32[]{:S(2)}) async-start(bf16[8,256,512]{2,1,0:T(8,128)(2,1)} %bitcast.13), calls=%async_computation | async-start | bytes 4194304 | tf_op jit(solution)/shard_map/all_to_all | solution.py:295
Sparse Core Ops, SparseCore 0:
  212.7 97.1 all-gather.2

commit v2 on v1

--- a/solution.py
+++ b/solution.py
@@ -272,6 +272,218 @@
     )(tok, gate_w, up_w, left, gate_r, up_r, gate_m, up_m)
 
 
+def mix_kernel(
+    hid, down_w, left, right, mag, out,
+    H, W, R, M_s, M_r, F, G, A_s, B_s, C_s, A_r, B_r, C_r, D_s, D_r, sq, q_m, q_t, q_r,
+    own, hs, hr, ys, yr, fs, fr, ws, wr, ms, mr, as_, ar, bs, br, cs, cr, ds, dr, qs, qr,
+):
+    z, xlo, y, xhi, core = place()
+
+    def at(dz=0, dx=0, dy=0):
+        return device((z + dz) % 4, (xlo + dx) % 2, (y + dy) % 4, xhi, core)
+
+    mate = device(z, xlo, y, xhi, 1 - core)
+    across = device(z, xlo, y, 1 - xhi, core)
+    rows_peers = [(dz, dx) for dz in range(4) for dx in range(2)][1:]
+    greet([mate, across, at(dy=1), at(dy=3)] + [at(dz=dz, dx=dx) for dz, dx in rows_peers])
+    started = []
+
+    def go(copy):
+        copy.start()
+        started.append(copy)
+        return copy
+
+    h_in = go(send(hid, H.at[y, xhi], hs.at[0], hr.at[0], across))
+    y_in = [[None, None], [None, None]]
+    for s in range(2):
+        y_in[s][0] = go(send(hid, H.at[y, xhi], ys.at[s, 0], yr.at[s, 0], at(dy=1 if s == 0 else 3)))
+    keep = pltpu.make_async_copy(hid, H.at[y, xhi], own.at[0])
+    keep.start()
+
+    w_in, w_own = [], []
+    w_in.append(go(send(right, R.at[core], ws.at[2], wr.at[2], mate)))
+    for xh in range(2):
+        theirs = pl.ds(pl.multiple_of((xh * 2 + 1 - core) * 896, 128), 896)
+        ours = pl.ds(pl.multiple_of((xh * 2 + core) * 896, 128), 896)
+        w_in.append(go(send(down_w.at[theirs], W.at[core, xh], ws.at[xh], wr.at[xh], mate)))
+        w_own.append(pltpu.make_async_copy(down_w.at[ours], W.at[core, xh], own.at[1 + xh]))
+    w_own.append(pltpu.make_async_copy(right, R.at[core], own.at[3]))
+    for copy in w_own:
+        copy.start()
+    for copy in w_own:
+        copy.wait()
+    for copy in w_in:
+        copy.wait_recv()
+    for cc in range(2):
+        sq[cc] = jnp.zeros((8, 512), jnp.float32)
+        for xh in range(2):
+
+            @pl.loop(0, 7)
+            def _(i):
+                part = pl.ds(pl.multiple_of(i * 128, 128), 128)
+                rows = pl.ds(pl.multiple_of((xh * 2 + core) * 896 + i * 128, 128), 128)
+                merged = W[cc, xh, part].astype(jnp.float32) + jnp.dot(
+                    left[rows], R[cc], preferred_element_type=jnp.float32
+                )
+                sq[cc] += jnp.sum((merged * merged).reshape(16, 8, 512), axis=0)
+                W[cc, xh, part] = merged.astype(jnp.bfloat16)
+
+    q_in = go(send(sq.at[1 - core], q_m, qs.at[7], qr.at[7], mate))
+    q_in.wait_recv()
+    q_t[...] = sq[core] + q_m[...]
+    row_in = []
+    for i, (dz, dx) in enumerate(rows_peers):
+        row_in.append(go(send(q_t, q_r.at[i], qs.at[i], qr.at[i], at(dz=dz, dx=dx))))
+
+    h_in.wait_recv()
+    for s in range(2):
+        block = H.at[y, 1 - xhi]
+        y_in[s][1] = go(send(block, block, ys.at[s, 1], yr.at[s, 1], at(dy=1 if s == 0 else 3)))
+
+    def pass_on(i):
+        xh = xhi if i == 0 else 1 - xhi
+        for s in range(2):
+            y_in[s][i].wait_recv()
+            part = H.at[(y + (3 if s == 0 else 1)) % 4, xh, pl.ds(4 * s, 4)]
+            send(part, part, fs.at[s, i], fr.at[s, i], at(dy=1 if s == 0 else 3)).start()
+
+    pass_on(0)
+    keep.wait()
+    for copy in row_in:
+        copy.wait_recv()
+    squares = q_t[...]
+    for i in range(7):
+        squares = squares + q_r[i]
+    scale = column_scale(mag[...], jnp.sum(squares, axis=0, keepdims=True))
+
+    def up_z(h):
+        return at(dz=1 if h == 0 else 3)
+
+    def down_z(h):
+        return at(dz=3 if h == 0 else 1)
+
+    def to_mate(i):
+        return send(M_s.at[i], M_r.at[i], ms.at[i], mr.at[i], mate)
+
+    def chain(i, h):
+        return send(A_s.at[i, h], A_r.at[i, h], as_.at[i, h], ar.at[i, h], up_z(h))
+
+    def direct(i, h):
+        return send(B_s.at[i, h], B_r.at[i, h], bs.at[i, h], br.at[i, h], down_z(h))
+
+    def last(i, h):
+        return send(C_s.at[i, h], C_r.at[i, h], cs.at[i, h], cr.at[i, h], up_z(h))
+
+    def aside(i):
+        return send(D_s.at[i], D_r.at[i], ds.at[i], dr.at[i], at(dx=1))
+
+    def block(i):
+        b = (y + 3 * i + 3 * (i // 2) + 2 * (i // 3)) % 4
+
+        def product(cc, n):
+            cols = pl.ds(pl.multiple_of(n * 256, 256), 256)
+            total = jnp.dot(
+                H[b, 0].reshape(512, 896), W[cc, 0, :, cols], preferred_element_type=jnp.float32
+            )
+            return total + jnp.dot(
+                H[b, 1].reshape(512, 896), W[cc, 1, :, cols], preferred_element_type=jnp.float32
+            )
+
+        @pl.loop(0, 2)
+        def _(n):
+            cols = pl.ds(pl.multiple_of(n * 256, 256), 256)
+            M_s[i, :, cols] = product(1 - core, n).astype(jnp.bfloat16)
+
+        to_mate(i).start()
+
+        @pl.loop(0, 2)
+        def _(n):
+            cols = pl.ds(pl.multiple_of(n * 256, 256), 256)
+            F[:, :, cols] = product(core, n).reshape(8, 64, 256)
+
+        to_mate(i).wait_recv()
+        F[...] += M_r[i].astype(jnp.float32).reshape(8, 64, 512)
+        for h in range(2):
+            A_s[i, h] = F[((z + 2) % 4) * 2 + h].astype(jnp.bfloat16)
+            chain(i, h).start()
+        for h in range(2):
+            B_s[i, h] = F[((z + (3 if h == 0 else 1)) % 4) * 2 + h].astype(jnp.bfloat16)
+            direct(i, h).start()
+        for h in range(2):
+            chain(i, h).wait_recv()
+            value = F[((z + (1 if h == 0 else 3)) % 4) * 2 + h] + A_r[i, h].astype(jnp.float32)
+            C_s[i, h] = value.astype(jnp.bfloat16)
+            last(i, h).start()
+        for h in range(2):
+            direct(i, h).wait_recv()
+            last(i, h).wait_recv()
+            G[h] = F[z * 2 + h] + B_r[i, h].astype(jnp.float32) + C_r[i, h].astype(jnp.float32)
+        D_s[i] = G[1 - xlo].astype(jnp.bfloat16)
+        aside(i).start()
+        aside(i).wait_recv()
+        total = (G[xlo] + D_r[i].astype(jnp.float32)) * scale
+        out[pl.ds(pl.multiple_of(b * 64, 64), 64), :] = total.astype(jnp.bfloat16)
+
+    @pl.loop(0, 4)
+    def _(i):
+        @pl.when(i == 1)
+        def _():
+            pass_on(1)
+
+        @pl.when(i == 3)
+        def _():
+            for s in range(2):
+                for k in range(2):
+                    part = H.at[(y + 2) % 4, (xhi, 1 - xhi)[k], pl.ds(4 * s, 4)]
+                    send(part, part, fs.at[s, k], fr.at[s, k], at(dy=1 if s == 0 else 3)).wait_recv()
+
+        block(i)
+
+    for copy in started:
+        copy.wait_send()
+    for s in range(2):
+        for k in range(2):
+            part = H.at[(y + (3 if s == 0 else 1)) % 4, (xhi, 1 - xhi)[k], pl.ds(4 * s, 4)]
+            send(part, part, fs.at[s, k], fr.at[s, k], at(dy=1 if s == 0 else 3)).wait_send()
+
+    @pl.loop(0, 4)
+    def _(i):
+        to_mate(i).wait_send()
+        aside(i).wait_send()
+        for h in range(2):
+            chain(i, h).wait_send()
+            direct(i, h).wait_send()
+            last(i, h).wait_send()
+
+
+def mixed_of(hid, down_w, left, right, mag):
+    anywhere = pl.BlockSpec(memory_space=pl.ANY)
+    vmem = pl.BlockSpec(memory_space=pltpu.VMEM)
+    dma = lambda *s: pltpu.SemaphoreType.DMA(s)
+    bf = lambda *s: pltpu.VMEM(s, jnp.bfloat16)
+    f32 = lambda *s: pltpu.VMEM(s, jnp.float32)
+    piece = lambda: bf(4, 2, 64, 512)
+    return pl.pallas_call(
+        mix_kernel,
+        out_shape=jax.ShapeDtypeStruct((256, 512), jnp.bfloat16),
+        in_specs=[vmem, anywhere, vmem, vmem, vmem],
+        out_specs=vmem,
+        scratch_shapes=[
+            bf(4, 2, 8, 64, 896), bf(2, 2, 896, 512), bf(2, 64, 512), bf(4, 512, 512), bf(4, 512, 512),
+            f32(8, 64, 512), f32(2, 64, 512),
+            piece(), piece(), piece(), piece(), piece(), piece(), bf(4, 64, 512), bf(4, 64, 512),
+            f32(2, 8, 512), f32(8, 512), f32(8, 512), f32(7, 8, 512),
+            dma(4), dma(1), dma(1), dma(2, 2), dma(2, 2), dma(2, 2), dma(2, 2), dma(3), dma(3),
+            dma(4), dma(4), dma(4, 2), dma(4, 2), dma(4, 2), dma(4, 2), dma(4, 2), dma(4, 2),
+            dma(4), dma(4), dma(8), dma(8),
+        ],
+        compiler_params=pltpu.CompilerParams(
+            collective_id=1, has_side_effects=True, vmem_limit_bytes=60 * 2**20
+        ),
+        name="mix_kernel",
+    )(hid, down_w, left, right, mag)
+
+
 def shards(
     tokens,
     gate_frozen_weight, gate_left_factor, gate_right_factor, gate_column_magnitude,
@@ -283,18 +495,9 @@
         tokens, gate_frozen_weight, up_frozen_weight, left, gate_right_factor, up_right_factor,
         gate_column_magnitude[None], up_column_magnitude[None],
     )
-    merged = down_frozen_weight.astype(jnp.float32) + jnp.dot(
-        down_left_factor, down_right_factor, preferred_element_type=jnp.float32
+    return mixed_of(
+        hidden, down_frozen_weight, down_left_factor, down_right_factor, down_column_magnitude[None]
     )
-    squares = jnp.sum(merged * merged, axis=0)
-    squares = lax.psum(squares, "row")
-    scale = column_scale(down_column_magnitude, squares)
-    full = lax.all_gather(hidden, "col", axis=0, tiled=False)
-    full = full.reshape(4, 4, 8, 64, 896).transpose(2, 0, 3, 1, 4).reshape(2048, 3584)
-    out = jnp.dot(full, merged.astype(jnp.bfloat16), preferred_element_type=jnp.float32)
-    tiles = lax.all_to_all(out.astype(jnp.bfloat16).reshape(8, 256, 512), "row", 0, 0, tiled=True)
-    mixed = jnp.sum(tiles.astype(jnp.float32), axis=0)
-    return (mixed * scale[None, :]).astype(jnp.bfloat16)
 
 
 def solution(mesh):

time: 396 us -> 303 us (0.77)
  waiting for transfers between devices: 92.2 us -> 0 us
  Pallas kernels: 201 us -> 293 us
  blocking collectives: 37.2 us -> 0 us
  local copies, waits for them, and re-layouts: 28.8 us -> 7.51 us
  matrix products: 17.1 us -> 0 us
  between operations: 13.5 us -> 0.04 us
  starting transfers between devices: 4.57 us -> 0 us
    all_gather x1 -> x0, waiting for transfers between devices: 92.2 us -> none  [shards(): full = lax.all_gather(hidden, 'col', axis=0, tiled=False)]
    pallas_call x0 -> x1, Pallas kernels: none -> 92 us  [mixed_of(): pl.pallas_call(mix_kernel, out_shape=jax.ShapeDtypeStruct((256, 512), jnp...]
    psum x1 -> x0, blocking collectives: 37.2 us -> none  [shards(): squares = lax.psum(squares, 'row')]
    dot_general x2 -> x0, matrix products: 17.1 us -> none  [the longest x1 12 us: shards(): jnp.dot(full, merged.astype(jnp.bfloat16), preferred_element_type=jnp.flo...]
    reshape x1 -> x0, local copies, waits for them, and re-layouts: 16.9 us -> none  [shards(): full.reshape(4, 4, 8, 64, 896).transpose(2, 0, 3, 1, 4).reshape(2048, 3584)]
    all_to_all x1 -> x0, starting transfers between devices: 4.57 us -> none  [shards(): lax.all_to_all(out.astype(jnp.bfloat16).reshape(8, 256, 512), 'row', 0, 0...]
    unnamed x11 -> x6, local copies, waits for them, and re-layouts: 9.2 us -> 4.87 us
  transfers between devices with their start and end apart: 2 -> 0, of which waited for: 1 -> 0; matrix products, arithmetic and copies ran while one was open for 1% -> 0% of each run, Pallas kernels for 0% -> 0%
where the time goes in v2:
time: 303 us; the launch traced here: 301 us
  Pallas kernels  293 us (97%)
  local copies, waits for them, and re-layouts  7.51 us (2%)
    pallas_call x1, Pallas kernels, hidden_of(): pl.pallas_call(hidden_kernel, out_shape=jax.ShapeDtypeStruct((8, 64, 896)...  201 us
    pallas_call x1, Pallas kernels, mixed_of(): pl.pallas_call(mix_kernel, out_shape=jax.ShapeDtypeStruct((256, 512), jnp...  92 us

profile of v2, /device:TPU:0, one launch (start us, length us, event | category | flops | bytes accessed | tf_op | source)
XLA Modules:
  0.0 300.9 jit_solution(12914649353632683098)
XLA Ops:
  0.0 1.3 broadcast_in_dim.9.gate_m
  1.3 1.3 broadcast_in_dim.10.up_m
  2.6 1.0 copy.14
  3.6 1.0 copy.15
  4.6 0.8 pad_maximum_fusion.left
  5.3 0.0 copy-start
  5.3 200.6 %hidden_kernel.1.hid = bf16[8,64,896]{2,1,0:T(8,128)(2,1)} custom-call(bf16[256,512]{1,0:T(8,128)(2,1)} %tok.1, bf16[512,3584]{1,0:T(8,128)(2,1)} %gate_w.1, bf16[512,3584]{1,0:T(8,128)(2,1)} %up_w.1, bf16[512,128]{1,0:T(8,128)(2,1)} %pad_maximum_fusion.left, bf16[64,3584]{1,0:T(8,128)(2,1)} %gate_r.1, bf16[64,3584]{1,0:T(8,128)(2,1)} %up_r.1, ...), custom_call_target="tpu_custom_call" | custom-call | tf_op jit(solution)/shard_map/hidden_kernel/pallas_call | solution.py:251
  206.0 0.0 copy-done
  206.0 1.3 copy.16.left
  207.2 92.0 %mix_kernel.1 = bf16[256,512]{1,0:T(8,128)(2,1)} custom-call(bf16[8,64,896]{2,1,0:T(8,128)(2,1)} %hidden_kernel.1.hid, bf16[3584,512]{1,0:T(8,128)(2,1)} %down_w.1, bf16[3584,64]{1,0:T(8,128)(2,1)} %copy.16.left, bf16[64,512]{1,0:T(8,128)(2,1)} %right.1, f32[1,512]{1,0:T(1,128)} %bitcast.1), custom_call_target="tpu_custom_call" | custom-call | tf_op jit(solution)/shard_map/mix_kernel/pallas_call | solution.py:466
  299.3 1.7 copy.18
Async XLA Ops:
  5.3 200.6 %copy-start = (bf16[3584,64]{0,1:T(8,128)(2,1)S(1)}, bf16[3584,64]{0,1:T(8,128)(2,1)}, u32[]{:S(2)}) copy-start(bf16[3584,64]{0,1:T(8,128)(2,1)} %param.23) | copy-start | bytes 1376260

commit v3 on v2

--- a/solution.py
+++ b/solution.py
@@ -112,7 +112,6 @@
         for copy in remote + local:
             copy.start()
 
-    fetch(0)
 
     for d in (1, 3, 2):
         x_in[d].wait_recv()
@@ -120,7 +119,6 @@
         z_in[0][d] = go(send(here, here, zs.at[0, d], zr.at[0, d], at_z(1)))
         z_in[1][d] = go(send(here, here, zs.at[1, d], zr.at[1, d], at_z(3)))
         d_in[0][d] = go(send(here, here, ds.at[0, d], dr.at[0, d], mate))
-    fetch(1)
     f_in = [[None] * 4, [None] * 4]
     for d in (0, 1, 3, 2):
         for s in range(2):
@@ -130,8 +128,6 @@
             f_in[s][d] = go(send(part, part, fs.at[s, d], fr.at[s, d], at_z(1 if s == 0 else 3)))
             here = tile(dz, d)
             d_in[1 + s][d] = go(send(here, here, ds.at[1 + s, d], dr.at[1 + s, d], mate))
-        if d in (0, 1, 3):
-            fetch((2, 3, None, 4)[d])
     for d in (0, 1, 3, 2):
         f_in[0][d].wait_recv()
         f_in[1][d].wait_recv()
@@ -139,6 +135,11 @@
         d_in[3][d] = go(send(here, here, ds.at[3, d], dr.at[3, d], mate))
     keep.wait()
     keep_l.wait()
+
+    @pl.loop(0, NJ)
+    def _(j):
+        fetch(j)
+
     for copy in l_in:
         copy.wait_recv()
     for i in range(4):
@@ -181,10 +182,6 @@
 
     @pl.loop(0, NJ)
     def _(j):
-        @pl.when(j < NJ - 5)
-        def _():
-            fetch(j + 5)
-
         local, remote = weight_copies(j)
         for copy in local:
             copy.wait()

time: 303 us -> 246 us (0.81)
  Pallas kernels: 293 us -> 238 us
    pallas_call x1, Pallas kernels: 201 us -> 144 us  [hidden_of(): pl.pallas_call(hidden_kernel, out_shape=jax.ShapeDtypeStruct((8, 64, 896)...]
where the time goes in v3:
time: 246 us
  Pallas kernels  238 us (97%)
  local copies, waits for them, and re-layouts  7.51 us (3%)
    pallas_call x1, Pallas kernels, hidden_of(): pl.pallas_call(hidden_kernel, out_shape=jax.ShapeDtypeStruct((8, 64, 896)...  144 us
    pallas_call x1, Pallas kernels, mixed_of(): pl.pallas_call(mix_kernel, out_shape=jax.ShapeDtypeStruct((256, 512), jnp...  93.9 us

profile of v3, /device:TPU:0, one launch (start us, length us, event | category | flops | bytes accessed | tf_op | source)
XLA Modules:
  0.0 245.9 jit_solution(16390305595156007337)
XLA Ops:
  0.0 1.3 broadcast_in_dim.9.gate_m
  1.3 1.3 broadcast_in_dim.10.up_m
  2.6 1.0 copy.14
  3.6 1.0 copy.15
  4.6 0.8 pad_maximum_fusion.left
  5.3 0.0 copy-start
  5.3 143.6 %hidden_kernel.1.hid = bf16[8,64,896]{2,1,0:T(8,128)(2,1)} custom-call(bf16[256,512]{1,0:T(8,128)(2,1)} %tok.1, bf16[512,3584]{1,0:T(8,128)(2,1)} %gate_w.1, bf16[512,3584]{1,0:T(8,128)(2,1)} %up_w.1, bf16[512,128]{1,0:T(8,128)(2,1)} %pad_maximum_fusion.left, bf16[64,3584]{1,0:T(8,128)(2,1)} %gate_r.1, bf16[64,3584]{1,0:T(8,128)(2,1)} %up_r.1, ...), custom_call_target="tpu_custom_call" | custom-call | tf_op jit(solution)/shard_map/hidden_kernel/pallas_call | solution.py:248
  149.0 0.0 copy-done
  149.0 1.3 copy.16.left
  150.2 93.9 %mix_kernel.1 = bf16[256,512]{1,0:T(8,128)(2,1)} custom-call(bf16[8,64,896]{2,1,0:T(8,128)(2,1)} %hidden_kernel.1.hid, bf16[3584,512]{1,0:T(8,128)(2,1)} %down_w.1, bf16[3584,64]{1,0:T(8,128)(2,1)} %copy.16.left, bf16[64,512]{1,0:T(8,128)(2,1)} %right.1, f32[1,512]{1,0:T(1,128)} %bitcast.1), custom_call_target="tpu_custom_call" | custom-call | tf_op jit(solution)/shard_map/mix_kernel/pallas_call | solution.py:463
  244.2 1.7 copy.18
Async XLA Ops:
  5.3 143.6 %copy-start = (bf16[3584,64]{0,1:T(8,128)(2,1)S(1)}, bf16[3584,64]{0,1:T(8,128)(2,1)}, u32[]{:S(2)}) copy-start(bf16[3584,64]{0,1:T(8,128)(2,1)} %param.23) | copy-start | bytes 1376260

commit v4 on v3

--- a/solution.py
+++ b/solution.py
@@ -128,6 +128,12 @@
             f_in[s][d] = go(send(part, part, fs.at[s, d], fr.at[s, d], at_z(1 if s == 0 else 3)))
             here = tile(dz, d)
             d_in[1 + s][d] = go(send(here, here, ds.at[1 + s, d], dr.at[1 + s, d], mate))
+        if d == 3:
+
+            @pl.loop(0, NJ)
+            def _(j):
+                fetch(j)
+
     for d in (0, 1, 3, 2):
         f_in[0][d].wait_recv()
         f_in[1][d].wait_recv()
@@ -135,11 +141,6 @@
         d_in[3][d] = go(send(here, here, ds.at[3, d], dr.at[3, d], mate))
     keep.wait()
     keep_l.wait()
-
-    @pl.loop(0, NJ)
-    def _(j):
-        fetch(j)
-
     for copy in l_in:
         copy.wait_recv()
     for i in range(4):
@@ -167,8 +168,8 @@
             copy.wait_recv()
         sq = jnp.sum(q_s[j] + q_r[j, 0] + q_r[j, 1] + q_r[j, 2], axis=0, keepdims=True)
         cols = pl.ds(pl.multiple_of(q * 896 + j * 128, 128), 128)
-        gate_scale = column_scale(gate_m[:, cols], sq[:, :128])
-        up_scale = column_scale(up_m[:, cols], sq[:, 128:])
+        gate_scale = column_scale(gate_m[cols][None], sq[:, :128])
+        up_scale = column_scale(up_m[cols][None], sq[:, 128:])
         for h in range(2):
             direct(j, h).wait_recv()
             last(j, h).wait_recv()
@@ -351,7 +352,7 @@
     squares = q_t[...]
     for i in range(7):
         squares = squares + q_r[i]
-    scale = column_scale(mag[...], jnp.sum(squares, axis=0, keepdims=True))
+    scale = column_scale(mag[...][None], jnp.sum(squares, axis=0, keepdims=True))
 
     def up_z(h):
         return at(dz=1 if h == 0 else 3)
@@ -490,10 +491,10 @@
     left = jnp.concatenate([gate_left_factor, up_left_factor], axis=1)
     hidden = hidden_of(
         tokens, gate_frozen_weight, up_frozen_weight, left, gate_right_factor, up_right_factor,
-        gate_column_magnitude[None], up_column_magnitude[None],
+        gate_column_magnitude, up_column_magnitude,
     )
     return mixed_of(
-        hidden, down_frozen_weight, down_left_factor, down_right_factor, down_column_magnitude[None]
+        hidden, down_frozen_weight, down_left_factor, down_right_factor, down_column_magnitude
     )
 
 

time: 246 us -> 231 us (0.939)
  Pallas kernels: 238 us -> 225 us
  local copies, waits for them, and re-layouts: 7.51 us -> 4.87 us
    pallas_call x1, Pallas kernels: 144 us -> 127 us  [hidden_of(): pl.pallas_call(hidden_kernel, out_shape=jax.ShapeDtypeStruct((8, 64, 896)...]
    pallas_call x1, Pallas kernels: 93.9 us -> 98.6 us  [mixed_of(): pl.pallas_call(mix_kernel, out_shape=jax.ShapeDtypeStruct((256, 512), jnp...]
    broadcast_in_dim x2 -> x0, local copies, waits for them, and re-layouts: 2.64 us -> none  [the longest x1 1.32 us: shards(): up_column_magnitude[None]]
where the time goes in v4:
time: 231 us
  Pallas kernels  225 us (97%)
  local copies, waits for them, and re-layouts  4.87 us (2%)
    pallas_call x1, Pallas kernels, hidden_of(): pl.pallas_call(hidden_kernel, out_shape=jax.ShapeDtypeStruct((8, 64, 896)...  127 us
    pallas_call x1, Pallas kernels, mixed_of(): pl.pallas_call(mix_kernel, out_shape=jax.ShapeDtypeStruct((256, 512), jnp...  98.6 us
    unnamed x6, local copies, waits for them, and re-layouts  4.87 us

profile of v4, /device:TPU:0, one launch (start us, length us, event | category | flops | bytes accessed | tf_op | source)
XLA Modules:
  0.0 230.9 jit_solution(746936899307133850)
XLA Ops:
  0.0 1.0 copy.14
  1.0 1.0 copy.15
  1.9 0.8 pad_maximum_fusion.left
  2.7 0.0 copy-start
  2.7 126.6 %hidden_kernel.1.hid = bf16[8,64,896]{2,1,0:T(8,128)(2,1)} custom-call(bf16[256,512]{1,0:T(8,128)(2,1)} %tok.1, bf16[512,3584]{1,0:T(8,128)(2,1)} %gate_w.1, bf16[512,3584]{1,0:T(8,128)(2,1)} %up_w.1, bf16[512,128]{1,0:T(8,128)(2,1)} %pad_maximum_fusion.left, bf16[64,3584]{1,0:T(8,128)(2,1)} %gate_r.1, bf16[64,3584]{1,0:T(8,128)(2,1)} %up_r.1, f32[3584]{0:T(1024)} %gate_m.1, ...), custom_call_target="tpu_custom_call" | custom-call | tf_op jit(solution)/shard_map/hidden_kernel/pallas_call | solution.py:249
  129.3 0.0 copy-done
  129.4 1.3 copy.16.left
  130.6 98.6 %mix_kernel.1 = bf16[256,512]{1,0:T(8,128)(2,1)} custom-call(bf16[8,64,896]{2,1,0:T(8,128)(2,1)} %hidden_kernel.1.hid, bf16[3584,512]{1,0:T(8,128)(2,1)} %down_w.1, bf16[3584,64]{1,0:T(8,128)(2,1)} %copy.16.left, bf16[64,512]{1,0:T(8,128)(2,1)} %right.1, f32[512]{0:T(512)} %mag.1), custom_call_target="tpu_custom_call" | custom-call | tf_op jit(solution)/shard_map/mix_kernel/pallas_call | solution.py:464
  229.3 1.7 copy.18
Async XLA Ops:
  2.7 126.6 %copy-start = (bf16[3584,64]{0,1:T(8,128)(2,1)S(1)}, bf16[3584,64]{0,1:T(8,128)(2,1)}, u32[]{:S(2)}) copy-start(bf16[3584,64]{0,1:T(8,128)(2,1)} %param.23) | copy-start | bytes 1376260

commit v5 on v4

--- a/solution.py
+++ b/solution.py
@@ -130,7 +130,7 @@
             d_in[1 + s][d] = go(send(here, here, ds.at[1 + s, d], dr.at[1 + s, d], mate))
         if d == 3:
 
-            @pl.loop(0, NJ)
+            @pl.loop(0, 3)
             def _(j):
                 fetch(j)
 
@@ -139,6 +139,11 @@
         f_in[1][d].wait_recv()
         here = tile(2, d)
         d_in[3][d] = go(send(here, here, ds.at[3, d], dr.at[3, d], mate))
+
+    @pl.loop(3, NJ)
+    def _(j):
+        fetch(j)
+
     keep.wait()
     keep_l.wait()
     for copy in l_in:

time: 231 us -> 231 us (level)
  no operation moved by 1% of the time
where the time goes in v5:
time: 231 us
  Pallas kernels  225 us (97%)
  local copies, waits for them, and re-layouts  4.87 us (2%)
    pallas_call x1, Pallas kernels, hidden_of(): pl.pallas_call(hidden_kernel, out_shape=jax.ShapeDtypeStruct((8, 64, 896)...  127 us
    pallas_call x1, Pallas kernels, mixed_of(): pl.pallas_call(mix_kernel, out_shape=jax.ShapeDtypeStruct((256, 512), jnp...  98.6 us
    unnamed x6, local copies, waits for them, and re-layouts  4.87 us

profile of v5, /device:TPU:0, one launch (start us, length us, event | category | flops | bytes accessed | tf_op | source)
XLA Modules:
  0.0 230.9 jit_solution(11272826062272036393)
XLA Ops:
  0.0 1.0 copy.14
  1.0 1.0 copy.15
  1.9 0.8 pad_maximum_fusion.left
  2.7 0.0 copy-start
  2.7 126.6 %hidden_kernel.1.hid = bf16[8,64,896]{2,1,0:T(8,128)(2,1)} custom-call(bf16[256,512]{1,0:T(8,128)(2,1)} %tok.1, bf16[512,3584]{1,0:T(8,128)(2,1)} %gate_w.1, bf16[512,3584]{1,0:T(8,128)(2,1)} %up_w.1, bf16[512,128]{1,0:T(8,128)(2,1)} %pad_maximum_fusion.left, bf16[64,3584]{1,0:T(8,128)(2,1)} %gate_r.1, bf16[64,3584]{1,0:T(8,128)(2,1)} %up_r.1, f32[3584]{0:T(1024)} %gate_m.1, ...), custom_call_target="tpu_custom_call" | custom-call | tf_op jit(solution)/shard_map/hidden_kernel/pallas_call | solution.py:254
  129.3 0.0 copy-done
  129.4 1.3 copy.16.left
  130.6 98.6 %mix_kernel.1 = bf16[256,512]{1,0:T(8,128)(2,1)} custom-call(bf16[8,64,896]{2,1,0:T(8,128)(2,1)} %hidden_kernel.1.hid, bf16[3584,512]{1,0:T(8,128)(2,1)} %down_w.1, bf16[3584,64]{1,0:T(8,128)(2,1)} %copy.16.left, bf16[64,512]{1,0:T(8,128)(2,1)} %right.1, f32[512]{0:T(512)} %mag.1), custom_call_target="tpu_custom_call" | custom-call | tf_op jit(solution)/shard_map/mix_kernel/pallas_call | solution.py:469
  229.3 1.7 copy.18
Async XLA Ops:
  2.7 126.6 %copy-start = (bf16[3584,64]{0,1:T(8,128)(2,1)S(1)}, bf16[3584,64]{0,1:T(8,128)(2,1)}, u32[]{:S(2)}) copy-start(bf16[3584,64]{0,1:T(8,128)(2,1)} %param.23) | copy-start | bytes 1376260
